TPU v7x, 32 devices: a 4x2x2 block of a 4x4x8 slice. The times are simulated.
32 devices in a mesh: dp: 4 (over y, z), sp: 8 (over x, core).
Axes of the slice: x: 4, y: 2, z: 2, core: 2. Of those that a mesh axis runs over, the one named last changes fastest.
The devices are a block of a 4x4x8 slice.
Arguments:
- dec_hidden: bfloat16 [4096, 768], P(('dp', 'sp')), parts along dimension 0
- enc_memory: bfloat16 [32768, 768], P(('dp', 'sp')), parts along dimension 0
- mem_len: int32 [4], P('dp'), parts along dimension 0
- norm_self: bfloat16 [2, 768], replicated
- norm_cross: bfloat16 [2, 768], replicated
- norm_mlp: bfloat16 [2, 768], replicated
- self_q: bfloat16 [2, 768, 768], replicated
- self_k: bfloat16 [2, 768, 768], replicated
- self_v: bfloat16 [2, 768, 768], replicated
- self_o: bfloat16 [2, 12, 64, 768], replicated
- cross_q: bfloat16 [2, 768, 768], replicated
- cross_k: bfloat16 [2, 768, 768], replicated
- cross_v: bfloat16 [2, 768, 768], replicated
- cross_o: bfloat16 [2, 12, 64, 768], replicated
- mlp_gate: bfloat16 [2, 768, 3072], replicated
- mlp_up: bfloat16 [2, 768, 3072], replicated
- mlp_down: bfloat16 [2, 3072, 768], replicated
Outputs:
- output: bfloat16 [4096, 768], P(('dp', 'sp')), parts along dimension 0
There are 4 independent parts. A program takes and returns all parts, laid end to end along the dimension named above; an argument that names none is the same for every part.
All inputs are finite; a program needn't handle non-finite values.
Results may differ from a plain program's by a relative error of at most 0.0154436.
Values are sent between devices in bfloat16 or wider.
A program may use at most 768 MiB of HBM per device.

v0:
```python
import jax
import jax.numpy as jnp
from jax import lax
from jax.sharding import PartitionSpec as P

EPS = 1e-6
NEG_BIG = -1e30


def rms_norm(hidden, gain_vec):
    hidden32 = hidden.astype(jnp.float32)
    inv_rms = lax.rsqrt(jnp.mean(hidden32 * hidden32, axis=-1, keepdims=True) + EPS)
    return (hidden32 * inv_rms * gain_vec.astype(jnp.float32)).astype(jnp.bfloat16)


def project(acts, weight_mat):
    return jnp.dot(acts, weight_mat, preferred_element_type=jnp.float32).astype(jnp.bfloat16)


def add_residual(hidden, update):
    return (hidden.astype(jnp.float32) + update).astype(jnp.bfloat16)


def solution(mesh):
    group = mesh.shape['sp']
    row_spec = P(('dp', 'sp'), None)

    def local_step(hidden, memory, mem_len, norm_self, norm_cross, norm_mlp, self_q, self_k, self_v, self_o, cross_q, cross_k, cross_v, cross_o, mlp_gate, mlp_up, mlp_down):
        rows, width = hidden.shape
        mem_rows = memory.shape[0]
        n_heads, head_dim = self_o.shape[1], self_o.shape[2]
        kv_heads = cross_k.shape[2] // head_dim
        n_groups = n_heads // kv_heads
        all_rows = rows * group
        soft_scale = head_dim ** -0.5
        shard_index = lax.axis_index('sp')
        query_pos = shard_index * rows + jnp.arange(rows)
        causal = query_pos[:, None] >= jnp.arange(all_rows)[None, :]
        mem_valid = (shard_index * mem_rows + jnp.arange(mem_rows)) < mem_len[0]
        for layer in range(norm_self.shape[0]):
            normed = rms_norm(hidden, norm_self[layer])
            queries = project(normed, self_q[layer]).reshape(rows, n_heads, head_dim)
            keys_all = lax.all_gather(project(normed, self_k[layer]), 'sp', axis=0, tiled=True).reshape(all_rows, n_heads, head_dim)
            values_all = lax.all_gather(project(normed, self_v[layer]), 'sp', axis=0, tiled=True).reshape(all_rows, n_heads, head_dim)
            scores = jnp.einsum('thd,shd->hts', queries, keys_all, preferred_element_type=jnp.float32) * soft_scale
            scores = jnp.where(causal, scores, NEG_BIG)
            weights = jnp.exp(scores - jnp.max(scores, axis=-1, keepdims=True))
            numerator = jnp.einsum('hts,shd->htd', weights.astype(jnp.bfloat16), values_all, preferred_element_type=jnp.float32)
            attended = (numerator / jnp.sum(weights, axis=-1, keepdims=True)).astype(jnp.bfloat16)
            hidden = add_residual(hidden, jnp.einsum('htd,hdo->to', attended, self_o[layer], preferred_element_type=jnp.float32))

            normed = rms_norm(hidden, norm_cross[layer])
            cross_queries = lax.all_gather(project(normed, cross_q[layer]), 'sp', axis=0, tiled=True).reshape(all_rows, kv_heads, n_groups, head_dim)
            mem_keys = project(memory, cross_k[layer]).reshape(mem_rows, kv_heads, head_dim)
            mem_values = project(memory, cross_v[layer]).reshape(mem_rows, kv_heads, head_dim)
            scores = jnp.einsum('tkgd,skd->kgts', cross_queries, mem_keys, preferred_element_type=jnp.float32) * soft_scale
            scores = jnp.where(mem_valid, scores, NEG_BIG)
            part_max = jnp.max(scores, axis=-1, keepdims=True)
            weights = jnp.exp(scores - part_max)
            part_sum = jnp.sum(weights, axis=-1, keepdims=True)
            part_num = jnp.einsum('kgts,skd->kgtd', weights.astype(jnp.bfloat16), mem_values, preferred_element_type=jnp.float32)
            rescale = jnp.exp(part_max - lax.pmax(part_max, 'sp'))
            packed = jnp.concatenate([part_num * rescale, part_sum * rescale], axis=-1)
            combined = lax.psum_scatter(packed, 'sp', scatter_dimension=2, tiled=True)
            attended = (combined[..., :head_dim] / combined[..., head_dim:]).astype(jnp.bfloat16)
            out_heads = cross_o[layer].reshape(kv_heads, n_groups, head_dim, width)
            hidden = add_residual(hidden, jnp.einsum('kgtd,kgdo->to', attended, out_heads, preferred_element_type=jnp.float32))

            normed = rms_norm(hidden, norm_mlp[layer])
            gate_pre = jnp.dot(normed, mlp_gate[layer], preferred_element_type=jnp.float32)
            up_proj = jnp.dot(normed, mlp_up[layer], preferred_element_type=jnp.float32)
            hidden_act = (jax.nn.silu(gate_pre) * up_proj).astype(jnp.bfloat16)
            hidden = add_residual(hidden, jnp.dot(hidden_act, mlp_down[layer], preferred_element_type=jnp.float32))
        return hidden

    return jax.shard_map(local_step, mesh=mesh, in_specs=(row_spec, row_spec, P('dp')) + (P(),) * 14, out_specs=row_spec, check_vma=False)
```

profile of v0, /device:TPU:80, one launch (start us, length us, event | category | flops | bytes accessed | tf_op | source)
XLA Modules:
  0.0 444.0 jit_solution(9772721656756068518)
XLA Ops:
  6.6 0.9 convert_reduce_fusion.2
  7.4 1.0 fusion.187
  8.5 2.4 fusion.113
  11.0 2.3 fusion.116
  13.5 1.6 fusion.110
  15.2 0.2 copy.26
  15.4 0.1 iota_compare_fusion
  15.5 19.6 %all-gather.7.cloned.1.call-done = bf16[1024,768]{1,0:T(8,128)(2,1)} async-done(((bf16[128,768]{1,0:T(8,128)(2,1)}), bf16[1024,768]{1,0:T(8,128)(2,1)}) %all-gather.7.cloned.1.call-update) | async-done | bytes 1572880 | tf_op jit(solution)/shard_map/all_gather | solution.py:43
  35.1 1.7 copy.27
  36.8 1.3 fusion.14
  38.1 2.7 copy-done.3
  40.8 1.7 fusion.16
  42.5 15.6 %all-gather.9.cloned.1.call-done = bf16[1024,768]{1,0:T(8,128)(2,1)} async-done(((bf16[128,768]{1,0:T(8,128)(2,1)}), bf16[1024,768]{1,0:T(8,128)(2,1)}) %all-gather.9.cloned.1.call-update) | async-done | bytes 1572880 | tf_op jit(solution)/shard_map/all_gather | solution.py:44
  58.1 1.7 copy.28
  59.8 5.8 %multiply_reduce_fusion.4 = (f32[128]{0:T(128)S(1)}, f32[128,768]{1,0:T(8,128)}) fusion(bf16[2,12,64,768]{3,2,1,0:T(8,128)(2,1)} %param.26, bf16[1024,12,64]{0,2,1:T(8,128)(2,1)S(1)} %bitcast.298, f32[12,128,1024]{2,1,0:T(8,128)} %copy-done.3, f32[12,128]{1,0:T(8,128)S(1)} %get-tuple-element.15, pred[128,1024]{1,0:T(8,128)(4,1)S(1)} %iota_compare_fusion, ...), kind=kOutput, calls=%fused_computation.154 | convolution fusion | flops 359399296 | bytes 9777664 | tf_op jit(solution)/shard_map/htd,hdo->to/dot_general | solution.py:50
  65.7 2.5 fusion.119
  68.2 0.4 reduce-scatter.3.cloned.1.call-start
  69.2 4.0 convolution_convert_fusion.3
  73.2 2.6 convolution_convert_fusion.2
  75.8 13.9 %all-gather.11.cloned.1.call-done = bf16[1024,768]{1,0:T(8,128)(2,1)} async-done(((bf16[128,768]{1,0:T(8,128)(2,1)}), bf16[1024,768]{1,0:T(8,128)(2,1)}) %all-gather.11.cloned.1.call-update) | async-done | bytes 1572880 | tf_op jit(solution)/shard_map/all_gather | solution.py:53
  89.7 1.7 copy.29
  91.4 20.1 %bitcast_reduce_fusion.1 = (f32[12,1024]{1,0:T(8,128)S(1)}, f32[12,1024,1024]{2,1,0:T(8,128)}) fusion(pred[1024]{0:T(1024)(128)(4,1)S(1)} %add_compare_fusion, bf16[1024,12,64]{0,2,1:T(8,128)(2,1)} %bitcast.295, bf16[1024,12,64]{0,2,1:T(8,128)(2,1)S(1)} %bitcast.291), kind=kOutput, calls=%fused_computation.5 | convolution fusion | flops 1648349184 | bytes 53527552 | tf_op jit(solution)/shard_map/tkgd,skd->kgts/dot_general | solution.py:56
  111.6 21.3 %fusion.2 = f32[12,1024]{1,0:T(8,128)S(1)} fusion(f32[12,1024,1024]{2,1,0:T(8,128)} %get-tuple-element.20, f32[12,1024]{1,0:T(8,128)S(1)} %get-tuple-element.19, pred[1024]{0:T(1024)(128)(4,1)S(1)} %add_compare_fusion), kind=kLoop, calls=%fused_computation.8 | loop fusion | flops 50319360 | bytes 50430976 | tf_op jit(solution)/shard_map/reduce_sum | solution.py:60
  132.9 24.7 %pmax.14 = f32[12,1,1024,1]{2,3,0,1:T(1,128)S(1)} all-reduce(f32[12,1,1024,1]{2,3,0,1:T(1,128)S(1)} %broadcast_in_dim.54), channel_id=1, replica_groups=mesh['dp'=4,'sp'=8] {'sp'}, use_global_device_ids=true, to_apply=%region_5.6 | all-reduce | flops 12288 | bytes 98304 | tf_op jit(solution)/shard_map/pmax | solution.py:62
  157.6 0.1 reshape_multiply_fusion.1
  157.8 18.8 %multiply_bitcast_fusion.1 = f32[12,1,1024,64]{2,3,0,1:T(8,128)S(1)} fusion(bf16[1024,12,64]{0,2,1:T(8,128)(2,1)} %bitcast.306, f32[12,1024,1024]{2,1,0:T(8,128)} %get-tuple-element.20, f32[12,1024]{1,0:T(8,128)S(1)} %get-tuple-element.19, pred[1024]{0:T(1024)(128)(4,1)S(1)} %add_compare_fusion, f32[12,1024]{1,0:T(8,128)S(1)} %bitcast.302), kind=kOutput, calls=%fused_computation.53 | convolution fusion | flops 1661730816 | bytes 55149568 | tf_op jit(solution)/shard_map/kgts,skd->kgtd/dot_general | solution.py:61
  176.6 2.0 pad_maximum_fusion
  178.7 0.6 all-gather.13.cloned.1.call-start
  179.4 31.9 %reduce-scatter.3.cloned.1.call-done = f32[12,1,128,65]{2,3,0,1:T(8,128)} async-done(((f32[12,1,1024,65]{2,3,0,1:T(8,128)}), f32[12,1,128,65]{2,3,0,1:T(8,128)}) %reduce-scatter.3.cloned.1.call-update) | async-done | bytes 399376 | tf_op jit(solution)/shard_map/reduce_scatter | solution.py:64
  211.2 0.8 slice.129
  212.0 1.8 multiply_reduce_fusion.3
  213.9 0.7 copy-done.4
  214.6 3.2 fusion.30
  217.8 6.3 %multiply_reduce_fusion.2 = (f32[128]{0:T(128)S(1)}, f32[128,768]{1,0:T(8,128)}) fusion(f32[128,768]{1,0:T(8,128)} %copy-done.4, bf16[2,3072,768]{2,1,0:T(8,128)(2,1)} %param.33, bf16[2,768,3072]{2,1,0:T(8,128)(2,1)} %param.32, f32[128,3072]{1,0:T(8,128)S(1)} %fusion.30, f32[768]{0:T(1024)S(1)} %get-tuple-element.6, f32[128]{0:T(128)S(1)} %add_rsqrt_fusion.3), kind=kOutput, calls=%fused_computation.150 | convolution fusion | flops 1211105152 | bytes 12193792 | tf_op jit(solution)/shard_map/dot_general | solution.py:73
  224.1 1.1 multiply_convert_fusion.2
  225.2 2.3 fusion.125
  227.6 2.3 fusion.128
  230.1 1.6 fusion.122
  231.7 0.2 copy.31
  231.8 15.9 %all-gather.13.cloned.1.call-done = bf16[1024,768]{1,0:T(8,128)(2,1)} async-done(((bf16[128,768]{1,0:T(8,128)(2,1)}), bf16[1024,768]{1,0:T(8,128)(2,1)}) %all-gather.13.cloned.1.call-update) | async-done | bytes 1572880 | tf_op jit(solution)/shard_map/all_gather | solution.py:43
  247.7 1.7 copy.32
  249.5 1.3 fusion.15
  250.7 2.7 copy-done.2
  253.4 1.7 fusion.18
  255.1 15.5 %all-gather.15.cloned.1.call-done = bf16[1024,768]{1,0:T(8,128)(2,1)} async-done(((bf16[128,768]{1,0:T(8,128)(2,1)}), bf16[1024,768]{1,0:T(8,128)(2,1)}) %all-gather.15.cloned.1.call-update) | async-done | bytes 1572880 | tf_op jit(solution)/shard_map/all_gather | solution.py:44
  270.6 1.7 copy.33
  272.3 5.9 %multiply_reduce_fusion.1 = (f32[128]{0:T(128)S(1)}, f32[128,768]{1,0:T(8,128)}) fusion(f32[128,768]{1,0:T(8,128)} %get-tuple-element.24, bf16[2,12,64,768]{3,2,1,0:T(8,128)(2,1)} %param.26, bf16[1024,12,64]{0,2,1:T(8,128)(2,1)S(1)} %bitcast.297, f32[12,128,1024]{2,1,0:T(8,128)} %copy-done.2, f32[12,128]{1,0:T(8,128)S(1)} %get-tuple-element.25, ...), kind=kOutput, calls=%fused_computation.148 | convolution fusion | flops 359300992 | bytes 9974272 | tf_op jit(solution)/shard_map/htd,hdo->to/dot_general | solution.py:50
  278.2 2.4 fusion.131
  280.7 0.2 reduce-scatter.5.cloned.1.call-start
  280.9 2.9 convolution_convert_fusion.1
  283.8 2.6 convolution_convert_fusion
  286.4 15.8 %all-gather.17.cloned.1.call-done = bf16[1024,768]{1,0:T(8,128)(2,1)} async-done(((bf16[128,768]{1,0:T(8,128)(2,1)}), bf16[1024,768]{1,0:T(8,128)(2,1)}) %all-gather.17.cloned.1.call-update) | async-done | bytes 1572880 | tf_op jit(solution)/shard_map/all_gather | solution.py:53
  302.2 1.7 copy.34
  303.9 20.4 %bitcast_reduce_fusion = (f32[12,1024]{1,0:T(8,128)S(1)}, f32[12,1024,1024]{2,1,0:T(8,128)}) fusion(pred[1024]{0:T(1024)(128)(4,1)S(1)} %add_compare_fusion, bf16[1024,12,64]{0,2,1:T(8,128)(2,1)S(1)} %bitcast.296, bf16[1024,12,64]{0,2,1:T(8,128)(2,1)S(1)} %bitcast.292), kind=kOutput, calls=%fused_computation.1 | convolution fusion | flops 1648349184 | bytes 53527552 | tf_op jit(solution)/shard_map/tkgd,skd->kgts/dot_general | solution.py:56
  324.4 21.4 %fusion.4 = f32[12,1024]{1,0:T(8,128)S(1)} fusion(f32[12,1024,1024]{2,1,0:T(8,128)} %get-tuple-element.30, f32[12,1024]{1,0:T(8,128)S(1)} %get-tuple-element.29, pred[1024]{0:T(1024)(128)(4,1)S(1)} %add_compare_fusion), kind=kLoop, calls=%fused_computation.10 | loop fusion | flops 50319360 | bytes 50430976 | tf_op jit(solution)/shard_map/reduce_sum | solution.py:60
  345.8 25.0 %pmax.15 = f32[12,1,1024,1]{2,3,0,1:T(1,128)S(1)} all-reduce(f32[12,1,1024,1]{2,3,0,1:T(1,128)S(1)} %broadcast_in_dim.56), channel_id=1, replica_groups=mesh['dp'=4,'sp'=8] {'sp'}, use_global_device_ids=true, to_apply=%region_14.15 | all-reduce | flops 12288 | bytes 98304 | tf_op jit(solution)/shard_map/pmax | solution.py:62
  370.8 0.1 reshape_multiply_fusion
  371.0 19.2 %multiply_bitcast_fusion = f32[12,1,1024,64]{2,3,0,1:T(8,128)S(1)} fusion(bf16[1024,12,64]{0,2,1:T(8,128)(2,1)S(1)} %bitcast.305, f32[12,1024,1024]{2,1,0:T(8,128)} %get-tuple-element.30, f32[12,1024]{1,0:T(8,128)S(1)} %get-tuple-element.29, pred[1024]{0:T(1024)(128)(4,1)S(1)} %add_compare_fusion, f32[12,1024]{1,0:T(8,128)S(1)} %bitcast.301), kind=kOutput, calls=%fused_computation.52 | convolution fusion | flops 1661730816 | bytes 55149568 | tf_op jit(solution)/shard_map/kgts,skd->kgtd/dot_general | solution.py:61
  390.2 2.0 pad_maximum_fusion.1
  392.3 32.5 %reduce-scatter.5.cloned.1.call-done = f32[12,1,128,65]{2,3,0,1:T(8,128)} async-done(((f32[12,1,1024,65]{2,3,0,1:T(8,128)}), f32[12,1,128,65]{2,3,0,1:T(8,128)}) %reduce-scatter.5.cloned.1.call-update) | async-done | bytes 399376 | tf_op jit(solution)/shard_map/reduce_scatter | solution.py:64
  424.8 0.8 slice.131
  425.6 1.8 multiply_reduce_fusion
  427.5 3.2 fusion.24
  430.7 6.2 %fusion.158 = bf16[128,768]{1,0:T(8,128)(2,1)} fusion(f32[128,768]{1,0:T(8,128)S(1)} %get-tuple-element.32, bf16[2,3072,768]{2,1,0:T(8,128)(2,1)} %param.33, bf16[2,768,3072]{2,1,0:T(8,128)(2,1)} %param.32, f32[128,3072]{1,0:T(8,128)S(1)} %fusion.24, f32[768]{0:T(1024)S(1)} %get-tuple-element.5, f32[128]{0:T(128)S(1)} %add_rsqrt_fusion), kind=kOutput, calls=%fused_computation.128 | convolution fusion | flops 1210810368 | bytes 11997696 | tf_op jit(solution)/shard_map/dot_general | solution.py:73
  (54 shorter events, 1.0 us)
Async XLA Ops:
  6.5 62.7 %copy-start = (bf16[1024,768]{1,0:T(8,128)(2,1)S(1)}, bf16[1024,768]{1,0:T(8,128)(2,1)}, u32[]{:S(2)}) copy-start(bf16[1024,768]{1,0:T(8,128)(2,1)} %param.18) | copy-start | bytes 4718596
  6.6 4.5 %copy-start.5 = (bf16[128,768]{1,0:T(8,128)(2,1)S(1)}, bf16[128,768]{1,0:T(8,128)(2,1)}, u32[]{:S(2)}) copy-start(bf16[128,768]{1,0:T(8,128)(2,1)} %param.17) | copy-start | bytes 589828
  6.6 28.6 %all-gather.7.cloned.1.call-start = ((), (), s32[]{:S(2)}) async-start(), calls=%async_computation.2 | async-start | bytes 1769472 | tf_op jit(solution)/shard_map/all_gather | solution.py:43
  10.9 4.4 %copy-start.7 = (bf16[2,768]{1,0:T(2,128)(2,1)S(1)}, bf16[2,768]{1,0:T(2,128)(2,1)}, u32[]{:S(2)}) copy-start(bf16[2,768]{1,0:T(2,128)(2,1)} %param.21) | copy-start | bytes 9220
  11.0 47.2 %all-gather.9.cloned.1.call-start = ((), (), s32[]{:S(2)}) async-start(), calls=%async_computation.3 | async-start | bytes 1769472 | tf_op jit(solution)/shard_map/all_gather | solution.py:44
  13.4 76.3 %all-gather.11.cloned.1.call-start = ((), (), s32[]{:S(2)}) async-start(), calls=%async_computation.4 | async-start | bytes 1769472 | tf_op jit(solution)/shard_map/all_gather | solution.py:53
  38.1 2.7 copy-start.3
  42.5 17.4 %copy-start.6 = (bf16[128,768]{1,0:T(8,128)(2,1)S(1)}, bf16[128,768]{1,0:T(8,128)(2,1)}, u32[]{:S(2)}) copy-start(bf16[128,768]{1,0:T(8,128)(2,1)} %param.17) | copy-start | bytes 589828
  68.2 143.0 %reduce-scatter.3.cloned.1.call-start = ((), (), s32[]{:S(2)}) async-start(), calls=%async_computation.5 | async-start | bytes 3981312 | tf_op jit(solution)/shard_map/reduce_scatter | solution.py:64
  69.2 4.0 copy-start.9
  178.7 0.7 copy-start.8
  178.7 33.4 %copy-start.12 = (f32[128,768]{1,0:T(8,128)S(1)}, f32[128,768]{1,0:T(8,128)}, u32[]{:S(2)}) copy-start(f32[128,768]{1,0:T(8,128)} %get-tuple-element.18) | copy-start | bytes 1179652
  178.7 69.0 %all-gather.13.cloned.1.call-start = ((), (), s32[]{:S(2)}) async-start(), calls=%async_computation.6 | async-start | bytes 1769472 | tf_op jit(solution)/shard_map/all_gather | solution.py:43
  213.9 0.7 copy-start.4
  227.6 43.0 %all-gather.15.cloned.1.call-start = ((), (), s32[]{:S(2)}) async-start(), calls=%async_computation.7 | async-start | bytes 1769472 | tf_op jit(solution)/shard_map/all_gather | solution.py:44
  230.0 72.2 %all-gather.17.cloned.1.call-start = ((), (), s32[]{:S(2)}) async-start(), calls=%async_computation.8 | async-start | bytes 1769472 | tf_op jit(solution)/shard_map/all_gather | solution.py:53
  250.7 2.7 copy-start.2
  280.7 144.1 %reduce-scatter.5.cloned.1.call-start = ((), (), s32[]{:S(2)}) async-start(), calls=%async_computation.9 | async-start | bytes 3981312 | tf_op jit(solution)/shard_map/reduce_scatter | solution.py:64
  280.9 2.9 copy-start.10
  324.4 46.6 %copy-start.11 = (bf16[1024,768]{0,1:T(8,128)(2,1)S(1)}, bf16[1024,768]{0,1:T(8,128)(2,1)}, u32[]{:S(2)}) copy-start(bf16[1024,768]{0,1:T(8,128)(2,1)} %convolution_convert_fusion) | copy-start | bytes 4718596
  392.2 33.4 %copy-start.13 = (f32[128,768]{1,0:T(8,128)S(1)}, f32[128,768]{1,0:T(8,128)}, u32[]{:S(2)}) copy-start(f32[128,768]{1,0:T(8,128)} %get-tuple-element.28) | copy-start | bytes 1179652
  430.6 6.3 %copy-start.1 = (bf16[1024,768]{1,0:T(8,128)(2,1)S(1)}, bf16[1024,768]{1,0:T(8,128)(2,1)}, u32[]{:S(2)}) copy-start(bf16[1024,768]{1,0:T(8,128)(2,1)} %param.18) | copy-start | bytes 4718596
Sparse Core Ops, SparseCore 0:
  11.1 23.9 all-gather.6
  36.7 21.3 all-gather.8
  68.3 21.3 all-gather.10
  178.8 32.3 reduce-scatter.2
  227.7 19.9 all-gather.12
  249.2 21.3 all-gather.14
  280.8 21.3 all-gather.16
  392.4 32.3 reduce-scatter.4
where the time goes:
time: 450 us; the launch traced here: 444 us
  waiting for transfers between devices  161 us (36%)
  matrix products  145 us (32%)
  other arithmetic  53.7 us (12%)
  blocking collectives  49.7 us (11%)
  local copies, waits for them, and re-layouts  18.4 us (4%)
  between operations  14.8 us (3%)
    reduce_scatter x2, waiting for transfers between devices, local_step(): combined = lax.psum_scatter(packed, 'sp', scatter_dimension=2, tiled=True)  64.4 us
    pmax x2, blocking collectives, local_step(): rescale = jnp.exp(part_max - lax.pmax(part_max, 'sp'))  49.7 us
    reduce_sum x2, other arithmetic, local_step(): part_sum = jnp.sum(weights, axis=-1, keepdims=True)  42.8 us
    dot_general x2, matrix products, local_step(): jnp.einsum('tkgd,skd->kgts', cross_queries, mem_keys, preferred_element_t...  40.5 us
    dot_general x2, matrix products, local_step(): jnp.einsum('kgts,skd->kgtd', weights.astype(jnp.bfloat16), mem_values, pr...  38 us
    all_gather x2, waiting for transfers between devices, local_step(): lax.all_gather(project(normed, self_k[layer]), 'sp', axis=0, tiled=True)  35.5 us
    all_gather x2, waiting for transfers between devices, local_step(): lax.all_gather(project(normed, self_v[layer]), 'sp', axis=0, tiled=True)  31.1 us
    all_gather x2, waiting for transfers between devices, local_step(): lax.all_gather(project(normed, cross_q[layer]), 'sp', axis=0, tiled=True)  29.7 us
  transfers between devices with their start and end apart: 8, of which 8 were waited for; matrix products, arithmetic and copies ran while one was open for 7% of the time, Pallas kernels for 0%

commit v1 on v0

v1 whole, which is shorter than its diff:
```python
import functools

import jax
import jax.numpy as jnp
from jax import lax
from jax.experimental import pallas as pl
from jax.experimental.pallas import tpu as pltpu
from jax.sharding import PartitionSpec as P

EPS = 1e-6
NEG_BIG = -1e30
LOG2E = 1.4426950408889634
F32 = jnp.float32
BF16 = jnp.bfloat16
MESH = pl.DeviceIdType.MESH


def rms_norm(hidden, gain_vec):
    hidden32 = hidden.astype(F32)
    inv_rms = lax.rsqrt(jnp.mean(hidden32 * hidden32, axis=-1, keepdims=True) + EPS)
    return (hidden32 * inv_rms * gain_vec.astype(F32)).astype(BF16)


def mm(a, b):
    return jnp.dot(a, b, preferred_element_type=F32)


def mm_nt(a, b):
    return lax.dot_general(a, b, (((1,), (1,)), ((), ())), preferred_element_type=F32)


def decoder_kernel(dims, *refs):
    (n_chips, layers, rows, width, heads, head_dim, mem_rows, ffl) = dims
    (hid_in, mem_in, mem_len, norm_self, norm_cross, norm_mlp,
     w_sq, w_sk, w_sv, w_so, w_cq, w_ck, w_cv, w_co, w_g, w_u, w_d, out,
     wsq, wsk, wsv, wso, wcq, wck, wcv, wco, wg, wu, wd,
     hbuf, mbuf, ybuf, wvt, qself, kself, vself, kc, vc, qc, s_even, s_odd,
     own_o, own_st, res_s, st_s, res_r, st_r, att, mlp_s, mlp_r,
     w_sem, l_sem, h_ss, h_rs, m_ss, m_rs, a_ss, a_rs, q_ss, q_rs, r_ss, r_rs, f_ss, f_rs) = refs
    T = 2 * rows
    half_w = width // 2
    hl = heads // 2
    pairs = hl // 2
    half = rows // 2
    mem_all = 2 * mem_rows
    exp_c = head_dim ** -0.5 * LOG2E
    neg = NEG_BIG * head_dim ** 0.5

    me = lax.axis_index("sp")
    c = me // 2
    h = me % 2
    sib = c * 2 + (1 - h)

    def peer(step):
        return lax.rem(c + step, n_chips) * 2 + h

    right, left, across = peer(1), peer(n_chips - 1), peer(2)
    back = (None, left, right, across)
    mirror = (0, 2, 1, 3)
    chip_of = (c, lax.rem(c + n_chips - 1, n_chips), lax.rem(c + 1, n_chips), lax.rem(c + 2, n_chips))

    def remote(src, dst, ss, rs, dev):
        return pltpu.make_async_remote_copy(src_ref=src, dst_ref=dst, send_sem=ss, recv_sem=rs,
                                            device_id={"sp": dev}, device_id_type=MESH)

    my_rows = pl.ds(pl.multiple_of(h * rows, rows), rows)
    sib_rows = pl.ds(pl.multiple_of((1 - h) * rows, rows), rows)
    my_a = pl.ds(pl.multiple_of(h * rows, half), half)
    my_b = pl.ds(pl.multiple_of(h * rows + half, half), half)
    my_cols = pl.ds(pl.multiple_of(h * half_w, 128), half_w)
    my_ff = pl.ds(pl.multiple_of(h * ffl, 128), ffl)

    hid_cp = pltpu.make_async_copy(hid_in, hbuf.at[0, 0, my_rows], l_sem.at[0])
    mem_cp = pltpu.make_async_copy(mem_in, mbuf.at[0], l_sem.at[1])
    hid_cp.start()
    mem_cp.start()

    plans = (
        (w_ck, wck, "c"), (w_cv, wcv, "c"), (w_sq, wsq, "c"), (w_sk, wsk, "c"), (w_sv, wsv, "c"), (w_so, wso, "f"),
        (w_cq, wcq, "c"), (w_co, wco, "f"), (w_g, wg, "m"), (w_u, wu, "m"), (w_d, wd, "r"),
    )
    CK, CV, SQ, SK, SV, SO, CQ, CO, G, U, DN = range(11)

    def w_copy(k, l):
        src, dst, kind = plans[k]
        if kind == "c":
            s = src.at[l, :, my_cols]
        elif kind == "m":
            s = src.at[l, :, my_ff]
        elif kind == "r":
            s = src.at[l, my_ff]
        else:
            s = src.at[l]
        return pltpu.make_async_copy(s, dst.at[l], w_sem.at[l, k])

    for l0 in range(layers):
        for k in range(len(plans)):
            w_copy(k, l0).start()

    barrier = pltpu.get_barrier_semaphore()
    for dev in (sib, right, left, across):
        pl.semaphore_signal(barrier, inc=1, device_id={"sp": dev}, device_id_type=MESH)
    pl.semaphore_wait(barrier, 4)

    def h_copy(l, k):
        spec = (
            (0, my_rows, 0, sib),
            (0, my_rows, 1, right),
            (0, my_rows, 2, left),
            (1, my_rows, 1, sib),
            (2, my_rows, 2, sib),
            (1, my_a, 3, right),
            (2, my_b, 3, left),
            (3, my_a, 3, sib),
            (3, my_b, 3, sib),
        )[k]
        s, rr, d, dev = spec
        return remote(hbuf.at[l, s, rr], hbuf.at[l, d, rr], h_ss.at[l, k], h_rs.at[l, k], dev)

    def h_recv(l, k):
        spec = ((0, sib_rows), (1, my_rows), (2, my_rows), (1, sib_rows), (2, sib_rows), (3, my_a), (3, my_b))
        if k < 7:
            s, rr = spec[k]
        else:
            off = (1 - h) * rows + (half if k == 8 else 0)
            s, rr = 3, pl.ds(pl.multiple_of(off, half), half)
        ref = hbuf.at[l, s, rr]
        return remote(ref, ref, h_ss.at[l, k], h_rs.at[l, k], sib)

    mem_send = remote(mbuf.at[0], mbuf.at[1], m_ss, m_rs, sib)

    def att_copy(l, k):
        ref = att.at[l, k, my_cols]
        return remote(ref, ref, a_ss.at[l, k], a_rs.at[l, k], sib)

    def q_copy(l, k):
        dev = (None, right, left, across)[k]
        return remote(qc.at[l, 0], qc.at[l, k], q_ss.at[l, k], q_rs.at[l, k], dev)

    def r_copy(l, k):
        return remote(res_s.at[l, k], res_r.at[l, mirror[k]], r_ss.at[l, 0, k], r_rs.at[l, 0, mirror[k]], back[k])

    def st_copy(l, k):
        return remote(st_s.at[l, k], st_r.at[l, mirror[k]], r_ss.at[l, 1, k], r_rs.at[l, 1, mirror[k]], back[k])

    def mlp_copy(l):
        return remote(mlp_s.at[l, sib_rows], mlp_r.at[l], f_ss.at[l], f_rs.at[l], sib)

    def attend(qref, kref, vref, nk, allowed, put):
        big = 512
        small = 256

        def rhs_of(pair, odd):
            start = pl.multiple_of(pair * 2 * head_dim + odd * head_dim, head_dim)
            q = qref[pl.ds(start, head_dim), :]
            z = jnp.zeros_like(q)
            return jnp.concatenate([z, q] if odd else [q, z], axis=0)

        def score(pair, rhs, s_ref, j, top):
            s = mm(kref[pair, j * big:(j + 1) * big, :], rhs)
            s = jnp.where(allowed(j * big, big), s, neg)
            s_ref[j * big:(j + 1) * big, :] = s
            t = jnp.max(s.reshape(big // 8, 8, T), axis=0)
            return t if top is None else jnp.maximum(top, t)

        def accumulate(head, s_ref, j, top, total, o):
            p = jnp.exp2((s_ref[j * small:(j + 1) * small, :] - top) * exp_c)
            t = jnp.sum(p.reshape(small // 8, 8, T), axis=0)
            v = mm(vref[head, :, j * small:(j + 1) * small], p.astype(BF16))
            return (t, v) if total is None else (total + t, o + v)

        def step(next_pair, next_odd, next_ref, head, cur_ref, cur_top):
            rhs = rhs_of(next_pair, next_odd)
            top = total = o = None
            for j in range(nk // big):
                top = score(next_pair, rhs, next_ref, j, top)
                for i in range(big // small):
                    total, o = accumulate(head, cur_ref, j * (big // small) + i, cur_top, total, o)
            put(head, o, cur_top, jnp.sum(total, axis=0, keepdims=True))
            return jnp.max(top, axis=0, keepdims=True)

        rhs0 = rhs_of(0, 0)
        top = None
        for j in range(nk // big):
            top = score(0, rhs0, s_even, j, top)
        top = jnp.max(top, axis=0, keepdims=True)

        def pair_body(pair, top_even):
            top_odd = step(pair, 1, s_odd, 2 * pair, s_even, top_even)
            return step(jnp.minimum(pair + 1, pairs - 1), 0, s_even, 2 * pair + 1, s_odd, top_odd)

        lax.fori_loop(0, pairs, pair_body, top)

    def gain(ref, l):
        g = ref[0:1, :].astype(F32)
        for i in range(1, layers):
            g = jnp.where(l == i, ref[i:i + 1, :].astype(F32), g)
        return g

    def project_t(x, w):
        return mm(x, w).astype(BF16).T

    def layer(l, carry):
        first = l == 0
        @pl.when(first)
        def _():
            hid_cp.wait()

        for k in range(3):
            h_copy(l, k).start()

        @pl.when(first)
        def _():
            mem_cp.wait()
            mem_send.start()

        w_copy(CK, l).wait()
        w_copy(CV, l).wait()
        wvt[...] = wcv[l].T
        blk = 512

        def mem_proj(part):
            def body(b, cc):
                r0 = pl.multiple_of(b * blk, blk)
                m = mbuf[part, pl.ds(r0, blk), :]
                k = mm(m, wck[l]).astype(BF16)
                d0 = pl.multiple_of(part * mem_rows + b * blk, blk)
                for p in range(pairs):
                    kc[p, pl.ds(d0, blk), :] = k[:, p * 128:(p + 1) * 128]
                v = mm_nt(wvt[...], m).astype(BF16)
                vc[:, :, pl.ds(d0, blk)] = v.reshape(hl, head_dim, blk)
                return cc

            lax.fori_loop(0, mem_rows // blk, body, 0)

        mem_proj(0)

        @pl.when(first)
        def _():
            mem_send.wait_recv()

        mem_proj(1)

        g_self = gain(norm_self, l)
        for k in (SQ, SK, SV):
            w_copy(k, l).wait()
        wvt[...] = wsv[l].T

        def self_proj(r, with_q):
            x = rms_norm(hbuf[l, r], g_self)
            if with_q:
                qself[...] = project_t(x, wsq[l])
            k = mm(x, wsk[l]).astype(BF16)
            for p in range(pairs):
                kself[p, r * T:(r + 1) * T, :] = k[:, p * 128:(p + 1) * 128]
            v = mm_nt(wvt[...], x).astype(BF16)
            vself[:, :, r * T:(r + 1) * T] = v.reshape(hl, head_dim, T)

        h_recv(l, 1).wait_recv()
        h_copy(l, 3).start()
        h_copy(l, 5).start()
        h_recv(l, 2).wait_recv()
        h_copy(l, 4).start()
        h_copy(l, 6).start()
        h_recv(l, 0).wait_recv()
        self_proj(0, True)
        h_recv(l, 3).wait_recv()
        self_proj(1, False)
        h_recv(l, 4).wait_recv()
        self_proj(2, False)
        h_recv(l, 5).wait_recv()
        h_copy(l, 7).start()
        h_recv(l, 6).wait_recv()
        h_copy(l, 8).start()
        h_recv(l, 7).wait_recv()
        h_recv(l, 8).wait_recv()
        self_proj(3, False)

        def causal(start, size):
            parts = []
            kio = lax.broadcasted_iota(jnp.int32, (T, T), 0)
            qio = lax.broadcasted_iota(jnp.int32, (T, T), 1)
            for r in range(start // T, (start + size) // T):
                parts.append(kio + (chip_of[r] - c) * T <= qio)
            return jnp.concatenate(parts, axis=0)

        def put_self(head, o, top, total):
            r0 = pl.multiple_of(h * half_w + head * head_dim, head_dim)
            att[l, 0, pl.ds(r0, head_dim), :] = (o / total).astype(BF16)

        attend(qself, kself, vself, n_chips * T, causal, put_self)
        att_copy(l, 0).start()
        w_copy(SO, l).wait()
        w_copy(CQ, l).wait()
        att_copy(l, 0).wait_recv()
        y = (hbuf[l, 0].astype(F32) + mm(att[l, 0].T, wso[l])).astype(BF16)
        ybuf[...] = y

        x = rms_norm(y, gain(norm_cross, l))
        qc[l, 0] = project_t(x, wcq[l])
        for k in range(1, 4):
            q_copy(l, k).start()
        limit = mem_len[0]

        def valid(start, size):
            core = h if start < mem_rows else 1 - h
            base = (2 * c + core) * mem_rows + start % mem_rows
            return lax.broadcasted_iota(jnp.int32, (size, T), 0) < limit - base

        def put_own(head, o, top, total):
            own_o[pl.ds(pl.multiple_of(head * head_dim, head_dim), head_dim), :] = o
            own_st[pl.ds(head, 1), :] = top
            own_st[pl.ds(8 + head, 1), :] = total

        attend(qc.at[l, 0], kc, vc, mem_all, valid, put_own)
        for r in (1, 2, 3):
            def put_far(head, o, top, total, r=r):
                res_s[l, r, pl.ds(pl.multiple_of(head * head_dim, head_dim), head_dim), :] = o.astype(BF16)
                st_s[l, r, pl.ds(head, 1), :] = top
                st_s[l, r, pl.ds(8 + head, 1), :] = total

            q_copy(l, r).wait_recv()
            attend(qc.at[l, r], kc, vc, mem_all, valid, put_far)
            r_copy(l, r).start()
            st_copy(l, r).start()

        for r in (1, 2, 3):
            r_copy(l, mirror[r]).wait_recv()
            st_copy(l, mirror[r]).wait_recv()
        for head in range(hl):
            hs = slice(head * head_dim, (head + 1) * head_dim)
            tops = [own_st[head:head + 1, :]] + [st_r[l, r, head:head + 1, :] for r in (1, 2, 3)]
            sums = [own_st[8 + head:9 + head, :]] + [st_r[l, r, 8 + head:9 + head, :] for r in (1, 2, 3)]
            nums = [own_o[hs, :]] + [res_r[l, r, hs, :].astype(F32) for r in (1, 2, 3)]
            top = functools.reduce(jnp.maximum, tops)
            scale = [jnp.exp2((t - top) * exp_c) for t in tops]
            den = sum(s * t for s, t in zip(scale, sums))
            num = sum(s * t for s, t in zip(scale, nums))
            r0 = pl.multiple_of(h * half_w + head * head_dim, head_dim)
            att[l, 1, pl.ds(r0, head_dim), :] = (num / den).astype(BF16)
        att_copy(l, 1).start()
        w_copy(CO, l).wait()
        w_copy(G, l).wait()
        w_copy(U, l).wait()
        w_copy(DN, l).wait()
        att_copy(l, 1).wait_recv()
        y = (ybuf[...].astype(F32) + mm(att[l, 1].T, wco[l])).astype(BF16)
        ybuf[...] = y

        x = rms_norm(y, gain(norm_mlp, l))
        step = 512
        acc = None
        for s in range(ffl // step):
            sl = slice(s * step, (s + 1) * step)
            gate = mm(x, wg[l, :, sl])
            act = (jax.nn.silu(gate) * mm(x, wu[l, :, sl])).astype(BF16)
            part = mm(act, wd[l, sl, :])
            acc = part if acc is None else acc + part
        mlp_s[l] = acc
        mlp_copy(l).start()
        mlp_copy(l).wait_recv()
        hbuf[l + 1, 0, my_rows, :] = (ybuf[my_rows, :].astype(F32) + (mlp_s[l, my_rows, :] + mlp_r[l])).astype(BF16)
        return carry

    lax.fori_loop(0, layers, layer, 0)
    out_cp = pltpu.make_async_copy(hbuf.at[layers, 0, my_rows], out, l_sem.at[2])
    out_cp.start()

    mem_send.wait_send()

    def drain(l, carry):
        for k in range(9):
            h_copy(l, k).wait_send()
        for k in range(2):
            att_copy(l, k).wait_send()
        for k in range(1, 4):
            q_copy(l, k).wait_send()
            r_copy(l, k).wait_send()
            st_copy(l, k).wait_send()
        mlp_copy(l).wait_send()
        return carry

    lax.fori_loop(0, layers, drain, 0)
    out_cp.wait()


def solution(mesh):
    group = mesh.shape["sp"]
    n_chips = group // 2
    row_spec = P(("dp", "sp"), None)

    def local_step(hidden, memory, mem_len, norm_self, norm_cross, norm_mlp, self_q, self_k, self_v, self_o, cross_q, cross_k, cross_v, cross_o, mlp_gate, mlp_up, mlp_down):
        rows, width = hidden.shape
        mem_rows = memory.shape[0]
        layers, heads, head_dim = self_o.shape[:3]
        ffl = mlp_gate.shape[2] // 2
        half_w = width // 2
        hl = heads // 2
        pairs = hl // 2
        T = 2 * rows
        mem_all = 2 * mem_rows
        wso = self_o.reshape(layers, heads * head_dim, width)
        wco = cross_o.reshape(layers, heads * head_dim, width)
        dims = (n_chips, layers, rows, width, heads, head_dim, mem_rows, ffl)
        dma = pltpu.SemaphoreType.DMA
        anyspace = pl.BlockSpec(memory_space=pl.ANY)
        vmem = pl.BlockSpec(memory_space=pltpu.VMEM)
        call = pl.pallas_call(
            functools.partial(decoder_kernel, dims),
            out_shape=jax.ShapeDtypeStruct(hidden.shape, BF16),
            in_specs=[anyspace, anyspace, pl.BlockSpec(memory_space=pltpu.SMEM)] + [vmem] * 3 + [anyspace] * 11,
            out_specs=anyspace,
            scratch_shapes=[
                pltpu.VMEM((layers, width, half_w), BF16),
                pltpu.VMEM((layers, width, half_w), BF16),
                pltpu.VMEM((layers, width, half_w), BF16),
                pltpu.VMEM((layers, width, width), BF16),
                pltpu.VMEM((layers, width, half_w), BF16),
                pltpu.VMEM((layers, width, half_w), BF16),
                pltpu.VMEM((layers, width, half_w), BF16),
                pltpu.VMEM((layers, width, width), BF16),
                pltpu.VMEM((layers, width, ffl), BF16),
                pltpu.VMEM((layers, width, ffl), BF16),
                pltpu.VMEM((layers, ffl, width), BF16),
                pltpu.VMEM((layers + 1, n_chips, T, width), BF16),
                pltpu.VMEM((2, mem_rows, width), BF16),
                pltpu.VMEM((T, width), BF16),
                pltpu.VMEM((half_w, width), BF16),
                pltpu.VMEM((half_w, T), BF16),
                pltpu.VMEM((pairs, n_chips * T, 128), BF16),
                pltpu.VMEM((hl, head_dim, n_chips * T), BF16),
                pltpu.VMEM((pairs, mem_all, 128), BF16),
                pltpu.VMEM((hl, head_dim, mem_all), BF16),
                pltpu.VMEM((layers, 4, half_w, T), BF16),
                pltpu.VMEM((mem_all, T), F32),
                pltpu.VMEM((mem_all, T), F32),
                pltpu.VMEM((half_w, T), F32),
                pltpu.VMEM((16, T), F32),
                pltpu.VMEM((layers, 4, half_w, T), BF16),
                pltpu.VMEM((layers, 4, 16, T), F32),
                pltpu.VMEM((layers, 4, half_w, T), BF16),
                pltpu.VMEM((layers, 4, 16, T), F32),
                pltpu.VMEM((layers, 2, width, T), BF16),
                pltpu.VMEM((layers, T, width), F32),
                pltpu.VMEM((layers, rows, width), F32),
                dma((layers, 11)),
                dma((3,)),
                dma((layers, 9)), dma((layers, 9)),
                dma, dma,
                dma((layers, 2)), dma((layers, 2)),
                dma((layers, 4)), dma((layers, 4)),
                dma((layers, 2, 4)), dma((layers, 2, 4)),
                dma((layers,)), dma((layers,)),
            ],
            compiler_params=pltpu.CompilerParams(collective_id=0, has_side_effects=True, vmem_limit_bytes=67043328),
            name="decoder",
        )
        return call(hidden, memory, mem_len, norm_self, norm_cross, norm_mlp, self_q, self_k, self_v, wso, cross_q, cross_k, cross_v, wco, mlp_gate, mlp_up, mlp_down)

    return jax.shard_map(local_step, mesh=mesh, in_specs=(row_spec, row_spec, P("dp")) + (P(),) * 14, out_specs=row_spec, check_vma=False)
```

time: 450 us -> 113 us (0.25)
  the two profiles are of different devices: /device:TPU:80 before, /device:TPU:84 now
where the time goes in v1:
time: 113 us
  Pallas kernels  110 us (97%)
  local copies, waits for them, and re-layouts  1.62 us (1%)
    pallas_call x1, Pallas kernels, local_step(): call(hidden, memory, mem_len, norm_self, norm_cross, norm_mlp, self_q, se...  110 us

profile of v1, /device:TPU:84, one launch (start us, length us, event | category | flops | bytes accessed | tf_op | source)
XLA Modules:
  0.0 112.7 jit_solution(1701455115581961005)
XLA Ops:
  0.7 110.4 %decoder.1 = bf16[128,768]{1,0:T(8,128)(2,1)} custom-call(bf16[128,768]{1,0:T(8,128)(2,1)} %refs_0_.1, bf16[1024,768]{1,0:T(8,128)(2,1)} %refs_1_.1, s32[1]{0:T(128)S(6)} %copy.19.refs_2_, bf16[2,768]{1,0:T(2,128)(2,1)} %refs_3_.1, bf16[2,768]{1,0:T(2,128)(2,1)} %refs_4_.1, bf16[2,768]{1,0:T(2,128)(2,1)} %refs_5_.1, bf16[2,768,768]{2,1,0:T(8,128)(2,1)} %refs_6_.1, ...), custom_call_target="tpu_custom_call" | custom-call | tf_op jit(solution)/shard_map/decoder/pallas_call | solution.py:458
  111.0 1.6 %copy.20 = bf16[128,768]{1,0:T(8,128)(2,1)} copy(bf16[128,768]{1,0:T(8,128)(2,1)} %decoder.1) | data formatting | bytes 393216

commit v2 on v1

v2 whole, which is shorter than its diff:
```python
import functools

import jax
import jax.numpy as jnp
from jax import lax
from jax.experimental import pallas as pl
from jax.experimental.pallas import tpu as pltpu
from jax.sharding import PartitionSpec as P

EPS = 1e-6
NEG_BIG = -1e30
LOG2E = 1.4426950408889634
F32 = jnp.float32
BF16 = jnp.bfloat16
MESH = pl.DeviceIdType.MESH
BIG = 512
SMALL = 256


def rms_norm(hidden, gain_vec):
    hidden32 = hidden.astype(F32)
    inv_rms = lax.rsqrt(jnp.mean(hidden32 * hidden32, axis=-1, keepdims=True) + EPS)
    return (hidden32 * inv_rms * gain_vec.astype(F32)).astype(BF16)


def mm(a, b):
    return jnp.dot(a, b, preferred_element_type=F32)


def mm_nt(a, b):
    return lax.dot_general(a, b, (((1,), (1,)), ((), ())), preferred_element_type=F32)


def decoder_kernel(dims, *refs):
    (n_chips, layers, rows, width, heads, head_dim, mem_rows, ffl) = dims
    (hid_in, mem_in, len_in, ns_in, nc_in, nm_in,
     w_sq, w_sk, w_sv, w_so, w_cq, w_ck, w_cv, w_co, w_g, w_u, w_d, out,
     wsq, wsk, wsv, wso, wcq, wck, wcv, wco, wg, wu, wd, norm_self, norm_cross, norm_mlp, mem_len,
     hbuf, mbuf, ybuf, wvt, qself, kself, vself, kc, vc, qc, s_even, s_odd,
     res_s, st_s, res_r, st_r, att, act, mlp_s, mlp_r,
     w_sem, l_sem, h_ss, h_rs, m_ss, m_rs, a_ss, a_rs, q_ss, q_rs, r_ss, r_rs, f_ss, f_rs) = refs
    T = 2 * rows
    half_w = width // 2
    hl = heads // 2
    pairs = hl // 2
    half = rows // 2
    pw = 2 * head_dim
    mem_all = 2 * mem_rows
    exp_c = head_dim ** -0.5 * LOG2E
    neg = NEG_BIG * LOG2E

    me = lax.axis_index("sp")
    c = me // 2
    h = me % 2
    sib = c * 2 + (1 - h)

    def peer(step):
        return lax.rem(c + step, n_chips) * 2 + h

    right, left, across = peer(1), peer(n_chips - 1), peer(2)
    chip_of = (c, lax.rem(c + n_chips - 1, n_chips), lax.rem(c + 1, n_chips), lax.rem(c + 2, n_chips))

    def remote(src, dst, ss, rs, dev):
        return pltpu.make_async_remote_copy(src_ref=src, dst_ref=dst, send_sem=ss, recv_sem=rs,
                                            device_id={"sp": dev}, device_id_type=MESH)

    def piece(core, part):
        return pl.ds(pl.multiple_of(core * rows + part * half, half), half)

    my_rows = pl.ds(pl.multiple_of(h * rows, rows), rows)
    sib_rows = pl.ds(pl.multiple_of((1 - h) * rows, rows), rows)
    my_cols = pl.ds(pl.multiple_of(h * half_w, 128), half_w)
    my_ff = pl.ds(pl.multiple_of(h * ffl, 128), ffl)

    plans = (
        (w_ck, wck, "c"), (w_cv, wcv, "c"), (w_sk, wsk, "c"), (w_sv, wsv, "c"), (w_sq, wsq, "c"), (w_so, wso, "f"),
        (w_cq, wcq, "c"), (w_co, wco, "f"), (w_g, wg, "m"), (w_u, wu, "m"), (w_d, wd, "r"),
    )
    CK, CV, SK, SV, SQ, SO, CQ, CO, G, U, DN = range(11)

    def w_copy(k, l):
        src, dst, kind = plans[k]
        if kind == "c":
            s = src.at[l, :, my_cols]
        elif kind == "m":
            s = src.at[l, :, my_ff]
        elif kind == "r":
            s = src.at[l, my_ff]
        else:
            s = src.at[l]
        return pltpu.make_async_copy(s, dst.at[l], w_sem.at[l, k])

    hid_cp = pltpu.make_async_copy(hid_in, hbuf.at[0, 0, my_rows], l_sem.at[0])
    mem_cp = pltpu.make_async_copy(mem_in, mbuf.at[0], l_sem.at[1])
    small = [pltpu.make_async_copy(s, d, l_sem.at[3 + i]) for i, (s, d) in enumerate(
        ((ns_in, norm_self), (nc_in, norm_cross), (nm_in, norm_mlp), (len_in, mem_len)))]
    hid_cp.start()
    mem_cp.start()
    w_copy(CK, 0).start()
    w_copy(CV, 0).start()
    for cp in small:
        cp.start()

    barrier = pltpu.get_barrier_semaphore()
    for dev in (sib, right, left, across):
        pl.semaphore_signal(barrier, inc=1, device_id={"sp": dev}, device_id_type=MESH)
    pl.semaphore_wait(barrier, 4)

    h_plan = (
        (0, 0, None, sib),
        (0, 1, 0, right), (0, 2, 1, left), (0, 1, 1, right), (0, 2, 0, left),
        (1, 3, 0, right), (2, 3, 1, left),
        (1, 1, None, sib), (2, 2, None, sib), (3, 3, 0, sib), (3, 3, 1, sib),
    )
    n_h = len(h_plan)

    def h_copy(l, k):
        s, d, part, dev = h_plan[k]
        rr = my_rows if part is None else piece(h, part)
        return remote(hbuf.at[l, s, rr], hbuf.at[l, d, rr], h_ss.at[l, k], h_rs.at[l, k], dev)

    def h_wait(l, k):
        s, d, part, dev = h_plan[k]
        core = 1 - h if k in (0, 7, 8, 9, 10) else h
        rr = pl.ds(pl.multiple_of(core * rows, rows), rows) if part is None else piece(core, part)
        ref = hbuf.at[l, d, rr]
        remote(ref, ref, h_ss.at[l, k], h_rs.at[l, k], sib).wait_recv()

    mem_send = remote(mbuf.at[0], mbuf.at[1], m_ss, m_rs, sib)

    def att_copy(l, k, p):
        ref = att.at[l, k, pl.ds(pl.multiple_of(h * half_w + p * pw, pw), pw)]
        return remote(ref, ref, a_ss.at[l, k, p], a_rs.at[l, k, p], sib)

    def att_wait(l, k, p):
        ref = att.at[l, k, pl.ds(pl.multiple_of((1 - h) * half_w + p * pw, pw), pw)]
        remote(ref, ref, a_ss.at[l, k, p], a_rs.at[l, k, p], sib).wait_recv()

    def pair_rows(p):
        return pl.ds(pl.multiple_of(p * pw, pw), pw)

    def q_copy(l, k, p):
        dev = (None, right, left, across)[k]
        return remote(qc.at[l, 0, pair_rows(p)], qc.at[l, k, pair_rows(p)], q_ss.at[l, k, p], q_rs.at[l, k, p], dev)

    def q_wait(l, k, p):
        ref = qc.at[l, k, pair_rows(p)]
        remote(ref, ref, q_ss.at[l, k, p], q_rs.at[l, k, p], sib).wait_recv()

    def r_copies(l, k, p):
        k = jnp.int32(k)
        step = jnp.where(k == 1, n_chips - 1, jnp.where(k == 2, 1, 2))
        slot = jnp.where(k == 1, 2, jnp.where(k == 2, 1, 3))
        dev = peer(step)
        return (remote(res_s.at[l, k, pair_rows(p)], res_r.at[l, slot, pair_rows(p)], r_ss.at[l, 0, k, p], r_rs.at[l, 0, slot, p], dev),
                remote(st_s.at[l, k, p], st_r.at[l, slot, p], r_ss.at[l, 1, k, p], r_rs.at[l, 1, slot, p], dev))

    def r_wait(l, k, p):
        a, b = res_r.at[l, k, pair_rows(p)], st_r.at[l, k, p]
        remote(a, a, r_ss.at[l, 0, k, p], r_rs.at[l, 0, k, p], sib).wait_recv()
        remote(b, b, r_ss.at[l, 1, k, p], r_rs.at[l, 1, k, p], sib).wait_recv()

    def mlp_copy(l):
        return remote(mlp_s.at[l], mlp_r.at[l], f_ss.at[l], f_rs.at[l], sib)

    def attend(items, item, qref, kref, vref, nk, allowed, before, put, after):
        def rhs_of(t, odd):
            block, pair = item(t)
            start = pl.multiple_of(pair * pw + odd * head_dim, head_dim)
            q = qref[block, pl.ds(start, head_dim), :].astype(F32) * exp_c
            hi = q.astype(BF16)
            lo = (q - hi.astype(F32)).astype(BF16)
            z = jnp.zeros_like(hi)
            return jnp.concatenate([z, hi, z, lo] if odd else [hi, z, lo, z], axis=0)

        def score(pair, rhs, s_ref, j, top):
            k = kref[pair, j * BIG:(j + 1) * BIG, :]
            s = mm(jnp.concatenate([k, k], axis=1), rhs)
            s = jnp.where(allowed(j * BIG, BIG), s, neg)
            s_ref[j * BIG:(j + 1) * BIG, :] = s
            t = jnp.max(s.reshape(BIG // 8, 8, T), axis=0)
            return t if top is None else jnp.maximum(top, t)

        def accumulate(head, s_ref, j, top, total, o):
            p = jnp.exp2(s_ref[j * SMALL:(j + 1) * SMALL, :] - top)
            t = jnp.sum(p.reshape(SMALL // 8, 8, T), axis=0)
            vt = jnp.concatenate([vref[head, j * (SMALL // 128) + i] for i in range(SMALL // 128)], axis=1)
            v = mm(vt, p.astype(BF16))
            return (t, v) if total is None else (total + t, o + v)

        def step(nxt, nxt_odd, nxt_ref, cur, cur_odd, cur_ref, cur_top):
            rhs = rhs_of(nxt, nxt_odd)
            nxt_pair = item(nxt)[1]
            head = item(cur)[1] * 2 + cur_odd
            top = total = o = None
            for j in range(nk // BIG):
                top = score(nxt_pair, rhs, nxt_ref, j, top)
                for i in range(BIG // SMALL):
                    total, o = accumulate(head, cur_ref, j * (BIG // SMALL) + i, cur_top, total, o)
            put(cur, cur_odd, o, cur_top, jnp.sum(total, axis=0, keepdims=True))
            return jnp.max(top, axis=0, keepdims=True)

        before(0)
        rhs0 = rhs_of(0, 0)
        top = None
        for j in range(nk // BIG):
            top = score(item(0)[1], rhs0, s_even, j, top)
        top = jnp.max(top, axis=0, keepdims=True)

        def body(t, top_even):
            last = t == items - 1
            nxt = jnp.where(last, t, t + 1)

            @pl.when(jnp.logical_not(last))
            def _():
                before(t + 1)

            top_odd = step(t, 1, s_odd, t, 0, s_even, top_even)
            top_next = step(nxt, 0, s_even, t, 1, s_odd, top_odd)
            after(t)
            return top_next

        lax.fori_loop(0, items, body, top)

    def gain(ref, l):
        g = ref[0:1, :].astype(F32)
        for i in range(1, layers):
            g = jnp.where(l == i, ref[i:i + 1, :].astype(F32), g)
        return g

    def store_kv(kref, vref, row0, tile0, k, v, n):
        for p in range(pairs):
            kref[p, pl.ds(row0, n), :] = k[:, p * pw:(p + 1) * pw]
        v = v.reshape(hl, head_dim, n)
        for i in range(n // 128):
            vref[:, pl.ds(tile0 + i, 1)] = v[:, None, :, i * 128:(i + 1) * 128]

    def layer(l, carry):
        first = l == 0
        with jax.named_scope("gather_send"):
            @pl.when(first)
            def _():
                hid_cp.wait()

            for k in range(5):
                h_copy(l, k).start()

            @pl.when(first)
            def _():
                mem_cp.wait()
                mem_send.start()
                for l0 in range(layers):
                    for k in range(len(plans)):
                        if l0 > 0 or k > CV:
                            w_copy(k, l0).start()

        with jax.named_scope("w_wait"):
            w_copy(CK, l).wait()
            w_copy(CV, l).wait()
            wvt[...] = wcv[l].T

        blk = 512

        def mem_proj(part):
            def body(b, cc):
                r0 = pl.multiple_of(b * blk, blk)
                m = mbuf[part, pl.ds(r0, blk), :]
                k = mm(m, wck[l]).astype(BF16)
                v = mm_nt(wvt[...], m).astype(BF16)
                d0 = pl.multiple_of(part * mem_rows + b * blk, blk)
                store_kv(kc, vc, d0, (part * mem_rows + b * blk) // 128, k, v, blk)
                return cc

            lax.fori_loop(0, mem_rows // blk, body, 0)

        with jax.named_scope("mem_proj0"):
            mem_proj(0)

            @pl.when(first)
            def _():
                mem_send.wait_recv()
                for cp in small:
                    cp.wait()

        with jax.named_scope("mem_proj1"):
            mem_proj(1)

        def self_proj(r, with_q):
            x = rms_norm(hbuf[l, r], gain(norm_self, l))
            k = mm(x, wsk[l]).astype(BF16)
            v = mm_nt(wvt[...], x).astype(BF16)
            store_kv(kself, vself, r * T, r * (T // 128), k, v, T)
            if with_q:
                qself[0] = mm(x, wsq[l]).astype(BF16).T

        with jax.named_scope("gather_wait1"):
            for k in (SK, SV, SQ):
                w_copy(k, l).wait()
            wvt[...] = wsv[l].T
            h_wait(l, 1)
            h_copy(l, 5).start()
            h_wait(l, 2)
            h_copy(l, 6).start()
            h_wait(l, 0)
        with jax.named_scope("self_proj0"):
            self_proj(0, True)
        with jax.named_scope("gather_wait2"):
            h_wait(l, 3)
            h_copy(l, 7).start()
            h_wait(l, 4)
            h_copy(l, 8).start()
            h_wait(l, 7)
        with jax.named_scope("self_proj1"):
            self_proj(1, False)
            h_wait(l, 8)
            self_proj(2, False)
        with jax.named_scope("gather_wait3"):
            h_wait(l, 5)
            h_copy(l, 9).start()
            h_wait(l, 6)
            h_copy(l, 10).start()
            h_wait(l, 9)
            h_wait(l, 10)
        with jax.named_scope("self_proj3"):
            self_proj(3, False)

        def causal(start, size):
            parts = []
            kio = lax.broadcasted_iota(jnp.int32, (T, T), 0)
            qio = lax.broadcasted_iota(jnp.int32, (T, T), 1)
            for r in range(start // T, (start + size) // T):
                parts.append(kio + (chip_of[r] - c) * T <= qio)
            return jnp.concatenate(parts, axis=0)

        def att_rows(t, odd):
            return pl.ds(pl.multiple_of(h * half_w + t * pw + odd * head_dim, head_dim), head_dim)

        def put_self(t, odd, o, top, total):
            att[l, 0, att_rows(t, odd), :] = (o / total).astype(BF16)

        with jax.named_scope("self_attend"):
            attend(pairs, lambda t: (0, t), qself, kself, vself, n_chips * T, causal, lambda t: None, put_self,
                   lambda t: att_copy(l, 0, t).start())
        with jax.named_scope("att0_exchange"):
            w_copy(SO, l).wait()
            w_copy(CQ, l).wait()
            for p in range(pairs):
                att_wait(l, 0, p)
        with jax.named_scope("self_o_q"):
            y = (hbuf[l, 0].astype(F32) + mm(att[l, 0].T, wso[l])).astype(BF16)
            ybuf[...] = y
            x = rms_norm(y, gain(norm_cross, l))
            qc[l, 0] = mm(x, wcq[l]).astype(BF16).T
            for p in range(pairs):
                for k in (1, 2):
                    q_copy(l, k, p).start()
            for p in range(pairs):
                q_copy(l, 3, p).start()

        limit = mem_len[0]

        def valid(start, size):
            core = h if start < mem_rows else 1 - h
            base = (2 * c + core) * mem_rows + start % mem_rows
            return lax.broadcasted_iota(jnp.int32, (size, T), 0) < limit - base

        n_items = 4 * pairs
        lead = pairs - 1

        def item(t):
            t = jnp.int32(t)
            u = t - lead
            far = jnp.logical_and(t >= lead, t < n_items - 1)
            block = jnp.where(far, 1 + u // pairs, 0)
            pair = jnp.where(far, u % pairs, jnp.where(t == n_items - 1, pairs - 1, t))
            return block, pair

        def before(t):
            block, pair = item(t)
            for k in (1, 2, 3):
                @pl.when(block == k)
                def _():
                    q_wait(l, k, pair)

        def put_cross(t, odd, o, top, total):
            block, pair = item(t)
            res_s[l, block, pl.ds(pl.multiple_of(pair * pw + odd * head_dim, head_dim), head_dim), :] = o.astype(BF16)
            st_s[l, block, pair, odd:odd + 1, :] = top
            st_s[l, block, pair, 2 + odd:3 + odd, :] = total

        def after(t):
            block, pair = item(t)

            @pl.when(block > 0)
            def _():
                for cp in r_copies(l, block, pair):
                    cp.start()

        with jax.named_scope("cross"):
            attend(n_items, item, qc.at[l], kc, vc, mem_all, valid, before, put_cross, after)

        for p in range(pairs):
            with jax.named_scope(f"res_wait{p}"):
                for r in (1, 2, 3):
                    r_wait(l, r, p)
            with jax.named_scope(f"combine{p}"):
                for odd in (0, 1):
                    hs = slice(p * pw + odd * head_dim, p * pw + (odd + 1) * head_dim)
                    tops = [st_s[l, 0, p, odd:odd + 1, :]] + [st_r[l, r, p, odd:odd + 1, :] for r in (1, 2, 3)]
                    sums = [st_s[l, 0, p, 2 + odd:3 + odd, :]] + [st_r[l, r, p, 2 + odd:3 + odd, :] for r in (1, 2, 3)]
                    nums = [res_s[l, 0, hs, :].astype(F32)] + [res_r[l, r, hs, :].astype(F32) for r in (1, 2, 3)]
                    top = functools.reduce(jnp.maximum, tops)
                    scale = [jnp.exp2(t - top) for t in tops]
                    den = sum(s * t for s, t in zip(scale, sums))
                    num = sum(s * t for s, t in zip(scale, nums))
                    att[l, 1, att_rows(p, odd), :] = (num / den).astype(BF16)
                att_copy(l, 1, p).start()
        with jax.named_scope("att1_exchange"):
            w_copy(CO, l).wait()
            w_copy(G, l).wait()
            w_copy(U, l).wait()
            w_copy(DN, l).wait()
            for p in range(pairs):
                att_wait(l, 1, p)
        with jax.named_scope("mlp"):
            y = (ybuf[...].astype(F32) + mm(att[l, 1].T, wco[l])).astype(BF16)
            ybuf[...] = y
            x = rms_norm(y, gain(norm_mlp, l))
            step = 512
            for s in range(ffl // step):
                sl = slice(s * step, (s + 1) * step)
                gate = mm(x, wg[l, :, sl])
                act[:, sl] = (jax.nn.silu(gate) * mm(x, wu[l, :, sl])).astype(BF16)
            mlp_s[l] = mm(act[sib_rows, :], wd[l])
            mlp_copy(l).start()
            mine = mm(act[my_rows, :], wd[l])
        with jax.named_scope("mlp_exchange"):
            remote(mlp_s.at[l], mlp_r.at[l], f_ss.at[l], f_rs.at[l], sib).wait_recv()
            hbuf[l + 1, 0, my_rows, :] = (ybuf[my_rows, :].astype(F32) + (mine + mlp_r[l])).astype(BF16)
        return carry

    lax.fori_loop(0, layers, layer, 0)
    out_cp = pltpu.make_async_copy(hbuf.at[layers, 0, my_rows], out, l_sem.at[2])
    out_cp.start()

    mem_send.wait_send()

    def drain(l, carry):
        for k in range(n_h):
            h_copy(l, k).wait_send()
        for p in range(pairs):
            for k in range(2):
                att_copy(l, k, p).wait_send()
            for k in range(1, 4):
                q_copy(l, k, p).wait_send()
                for cp in r_copies(l, k, p):
                    cp.wait_send()
        mlp_copy(l).wait_send()
        return carry

    lax.fori_loop(0, layers, drain, 0)
    out_cp.wait()


def solution(mesh):
    group = mesh.shape["sp"]
    n_chips = group // 2
    row_spec = P(("dp", "sp"), None)

    def local_step(hidden, memory, mem_len, norm_self, norm_cross, norm_mlp, self_q, self_k, self_v, self_o, cross_q, cross_k, cross_v, cross_o, mlp_gate, mlp_up, mlp_down):
        rows, width = hidden.shape
        mem_rows = memory.shape[0]
        layers, heads, head_dim = self_o.shape[:3]
        ffl = mlp_gate.shape[2] // 2
        half_w = width // 2
        hl = heads // 2
        pairs = hl // 2
        T = 2 * rows
        mem_all = 2 * mem_rows
        wso = self_o.reshape(layers, heads * head_dim, width)
        wco = cross_o.reshape(layers, heads * head_dim, width)
        dims = (n_chips, layers, rows, width, heads, head_dim, mem_rows, ffl)
        dma = pltpu.SemaphoreType.DMA
        anyspace = pl.BlockSpec(memory_space=pl.ANY)
        call = pl.pallas_call(
            functools.partial(decoder_kernel, dims),
            out_shape=jax.ShapeDtypeStruct(hidden.shape, BF16),
            in_specs=[anyspace] * 17,
            out_specs=anyspace,
            scratch_shapes=[
                pltpu.VMEM((layers, width, half_w), BF16),
                pltpu.VMEM((layers, width, half_w), BF16),
                pltpu.VMEM((layers, width, half_w), BF16),
                pltpu.VMEM((layers, width, width), BF16),
                pltpu.VMEM((layers, width, half_w), BF16),
                pltpu.VMEM((layers, width, half_w), BF16),
                pltpu.VMEM((layers, width, half_w), BF16),
                pltpu.VMEM((layers, width, width), BF16),
                pltpu.VMEM((layers, width, ffl), BF16),
                pltpu.VMEM((layers, width, ffl), BF16),
                pltpu.VMEM((layers, ffl, width), BF16),
                pltpu.VMEM((layers, width), BF16),
                pltpu.VMEM((layers, width), BF16),
                pltpu.VMEM((layers, width), BF16),
                pltpu.SMEM((1,), jnp.int32),
                pltpu.VMEM((layers + 1, n_chips, T, width), BF16),
                pltpu.VMEM((2, mem_rows, width), BF16),
                pltpu.VMEM((T, width), BF16),
                pltpu.VMEM((half_w, width), BF16),
                pltpu.VMEM((1, half_w, T), BF16),
                pltpu.VMEM((pairs, n_chips * T, 128), BF16),
                pltpu.VMEM((hl, n_chips * T // 128, head_dim, 128), BF16),
                pltpu.VMEM((pairs, mem_all, 128), BF16),
                pltpu.VMEM((hl, mem_all // 128, head_dim, 128), BF16),
                pltpu.VMEM((layers, 4, half_w, T), BF16),
                pltpu.VMEM((mem_all, T), F32),
                pltpu.VMEM((mem_all, T), F32),
                pltpu.VMEM((layers, 4, half_w, T), BF16),
                pltpu.VMEM((layers, 4, pairs, 8, T), F32),
                pltpu.VMEM((layers, 4, half_w, T), BF16),
                pltpu.VMEM((layers, 4, pairs, 8, T), F32),
                pltpu.VMEM((layers, 2, width, T), BF16),
                pltpu.VMEM((T, ffl), BF16),
                pltpu.VMEM((layers, rows, width), F32),
                pltpu.VMEM((layers, rows, width), F32),
                dma((layers, 11)),
                dma((7,)),
                dma((layers, 11)), dma((layers, 11)),
                dma, dma,
                dma((layers, 2, pairs)), dma((layers, 2, pairs)),
                dma((layers, 4, pairs)), dma((layers, 4, pairs)),
                dma((layers, 2, 4, pairs)), dma((layers, 2, 4, pairs)),
                dma((layers,)), dma((layers,)),
            ],
            compiler_params=pltpu.CompilerParams(collective_id=0, has_side_effects=True, vmem_limit_bytes=67043328),
            name="decoder",
        )
        return call(hidden, memory, mem_len, norm_self, norm_cross, norm_mlp, self_q, self_k, self_v, wso, cross_q, cross_k, cross_v, wco, mlp_gate, mlp_up, mlp_down)

    return jax.shard_map(local_step, mesh=mesh, in_specs=(row_spec, row_spec, P("dp")) + (P(),) * 14, out_specs=row_spec, check_vma=False)
```

time: 113 us -> 102 us (0.903)
  the two profiles are of different devices: /device:TPU:84 before, /device:TPU:80 now
where the time goes in v2:
time: 102 us; the launch traced here: 101 us
  Pallas kernels  98.6 us (97%)
  local copies, waits for them, and re-layouts  1.62 us (2%)
    pallas_call x1, Pallas kernels, local_step(): call(hidden, memory, mem_len, norm_self, norm_cross, norm_mlp, self_q, se...  98.6 us

profile of v2, /device:TPU:80, one launch (start us, length us, event | category | flops | bytes accessed | tf_op | source)
XLA Modules:
  0.0 100.9 jit_solution(17561848979638267972)
XLA Ops:
  0.7 98.6 %decoder.1 = bf16[128,768]{1,0:T(8,128)(2,1)} custom-call(bf16[128,768]{1,0:T(8,128)(2,1)} %refs_0_.1, bf16[1024,768]{1,0:T(8,128)(2,1)} %refs_1_.1, s32[1]{0:T(128)S(6)} %copy.19.refs_2_, bf16[2,768]{1,0:T(2,128)(2,1)} %refs_3_.1, bf16[2,768]{1,0:T(2,128)(2,1)} %refs_4_.1, bf16[2,768]{1,0:T(2,128)(2,1)} %refs_5_.1, bf16[2,768,768]{2,1,0:T(8,128)(2,1)} %refs_6_.1, ...), custom_call_target="tpu_custom_call" | custom-call | tf_op jit(solution)/shard_map/decoder/pallas_call | solution.py:538
  99.3 1.6 %copy.20 = bf16[128,768]{1,0:T(8,128)(2,1)} copy(bf16[128,768]{1,0:T(8,128)(2,1)} %decoder.1) | data formatting | bytes 393216
